TPU v7x, 32 devices: a whole 2x2x4 slice. The times are simulated.
32 devices in a mesh: dp: 8 (over y, x, core), mp: 4 (over z).
Axes of the slice: x: 2, y: 2, z: 4, core: 2. Of those that a mesh axis runs over, the one named last changes fastest.
Arguments:
- hidden: bfloat16 [4096, 16384], P('dp', 'mp'), may hold values from -64 to 64
- key_weight: bfloat16 [16384, 1024], P(('mp', 'dp')), may hold values from -0.046875 to 0.046875
- key_state: float32 [16384], P(('mp', 'dp')), may hold values from 2.9802323e-09 to 1.1920929e-07
- key_cotangent: bfloat16 [4096, 1024], P('dp'), may hold values from -6 to 6
- doc_lengths: int32 [16, 4], P('dp'), may hold values from 1 to 128, 256 in all within a row
Outputs:
- input_grad: bfloat16 [4096, 16384], P('dp', 'mp')
- new_weight: bfloat16 [16384, 1024], P(('mp', 'dp'))
- new_state: float32 [16384], P(('mp', 'dp'))
Inputs may be any that keep to these rules, and one draw needn't show every extreme that they name: `doc_lengths`: each row lists the lengths of the documents of one sequence, in order, summing to 256.
All inputs are finite; a program needn't handle non-finite values.
Results may differ from a plain program's by a relative error of at most 0.0045.
Values may be sent and summed in bfloat16 or wider, within the bound.
A program may use at most 128 MiB of HBM per device.

v0:
```python
import functools

import jax
import jax.numpy as jnp
from jax import lax
from jax.experimental import pallas as pl
from jax.experimental.pallas import tpu as pltpu
from jax.sharding import PartitionSpec as P

HD = 128
LEN = 256


learn_rate = 0.01


def positions_of(doc_lengths):
    doc_ends = jnp.cumsum(doc_lengths, axis=1)
    doc_starts = doc_ends - doc_lengths
    places = jnp.arange(LEN, dtype=jnp.int32)
    before = doc_starts[:, None, :] <= places[None, :, None]
    doc_start = jnp.max(jnp.where(before, doc_starts[:, None, :], 0), axis=2)
    return (places[None, :] - doc_start).reshape(-1)


def rope_back(cotangent, positions):
    half_dim = HD // 2
    frequency = jnp.exp(
        -(2.0 * jnp.arange(half_dim, dtype=jnp.float32) / HD) * jnp.log(jnp.float32(500000.0))
    )
    angles = positions.astype(jnp.float32)[:, None] * frequency[None, :]
    cos_part = jnp.cos(angles)[:, None, :]
    sin_part = jnp.sin(angles)[:, None, :]
    gradients = cotangent.astype(jnp.float32).reshape(cotangent.shape[0], -1, HD)
    first_half = gradients[..., :half_dim]
    second_half = gradients[..., half_dim:]
    rotated = jnp.concatenate(
        [
            first_half * cos_part + second_half * sin_part,
            second_half * cos_part - first_half * sin_part,
        ],
        axis=-1,
    )
    return rotated.reshape(cotangent.shape[0], -1).astype(jnp.bfloat16)


def update(owned, key_weight, key_state):
    squared = owned * owned
    squares_sum = lax.psum(jnp.sum(squared), ("dp", "mp"))
    clip_factor = jnp.minimum(jnp.float32(1.0), 1.0 / jnp.sqrt(squares_sum + 1e-06))
    row_mean = jnp.mean(squared, axis=1)
    new_state = key_state + clip_factor * clip_factor * row_mean
    step_size = learn_rate * clip_factor * owned / (jnp.sqrt(new_state)[:, None] + 1e-10)
    new_weight = (key_weight.astype(jnp.float32) - step_size).astype(jnp.bfloat16)
    return new_weight, new_state


def shards(hidden, key_weight, key_state, key_cotangent, doc_lengths):
    positions = positions_of(doc_lengths)
    key_grad = rope_back(key_cotangent, positions)
    gathered = lax.dot_general(
        key_grad,
        lax.all_gather(key_weight, "dp", axis=0, tiled=True),
        (((1,), (1,)), ((), ())),
        preferred_element_type=jnp.float32,
    )
    input_grad = gathered.astype(jnp.bfloat16)
    owned = lax.psum_scatter(
        lax.dot_general(
            hidden, key_grad, (((0,), (0,)), ((), ())), preferred_element_type=jnp.float32
        ),
        "dp",
        scatter_dimension=0,
        tiled=True,
    )
    return (input_grad, *update(owned, key_weight, key_state))


KG, HID, OWN_SIB, OWN_X, OWN_Y, RS1_X, RS1_Y, RS2_X, RS2_Y, FWD_X, FWD_Y, SIB_X, SIB_Y, SIB_D = (
    0, 1, 5, 6, 8, 10, 12, 14, 15, 16, 17, 18, 19, 20)
COPIES = 21


def exchange(zs, kg, hid, w, state, ig, new_w, new_state, g, squares, sums, got, wall, kgs, hs, part, s1x, s1y, r1x, r1y, s2x, s2y, r2x, r2y, send, recv, sum_send, sum_recv):
    f32 = jnp.float32
    rows = w.shape[0]
    half = rows // 2
    cols = kg.shape[1] // 2
    d = lax.axis_index("dp")
    core, xb, yb = lax.rem(d, 2), lax.rem(d // 2, 2), d // 4
    sib = d + 1 - 2 * core
    xn = d + 2 - 4 * xb
    yn = d + 4 - 8 * yb
    dg = xn + 4 - 8 * yb

    def sibling_of(block):
        return block + 1 - 2 * core

    def remote(place, src, dst, to):
        return pltpu.make_async_remote_copy(
            src_ref=src,
            dst_ref=dst,
            send_sem=send.at[place],
            recv_sem=recv.at[place],
            device_id={"dp": to},
            device_id_type=pl.DeviceIdType.MESH,
        )

    barrier = pltpu.get_barrier_semaphore()
    m = lax.axis_index("mp")
    partners = [{"mp": m + bit - 2 * bit * lax.rem(m // bit, 2)} for bit in zs]
    partners += [{"dp": sib}, {"dp": xn}, {"dp": yn}]
    for to in partners:
        pl.semaphore_signal(barrier, inc=1, device_id=to, device_id_type=pl.DeviceIdType.MESH)
    pl.semaphore_wait(barrier, len(partners))

    def columns(block, at=0, size=None):
        size = rows if size is None else size
        return pl.ds(pl.multiple_of(block * rows + at, size), size)

    copies = {}

    def begin(place, src, dst, to):
        copies[place] = remote(place, src, dst, to)
        copies[place].start()

    first, second = pl.ds(0, half), pl.ds(half, half)
    begin(OWN_X, w.at[first], wall.at[d, first], xn)
    begin(OWN_Y, w.at[first], wall.at[d, first], yn)
    begin(KG, kg, kgs, sib)
    blocks = (dg, xn, yn, d)
    for i, block in enumerate(blocks):
        begin(HID + i, hid.at[:, columns(sibling_of(block))], hs.at[i], sib)
    begin(OWN_SIB, w, wall.at[d], sib)

    def dot_t(a, b):
        return lax.dot_general(a, b, (((0,), (0,)), ((), ())), preferred_element_type=f32)

    for i, block in enumerate(blocks):

        @pl.loop(0, 2)
        def _(t, i=i, block=block):
            part[i, pl.ds(t * half, half), :] = dot_t(hid[:, columns(block, t * half, half)], kg[...])

    copies[KG].wait_recv()
    for i, block in enumerate(blocks):
        copies[HID + i].wait_recv()

        @pl.loop(0, 2)
        def _(t, i=i):
            at = pl.ds(t * half, half)
            total = part[i, at, :] + dot_t(hs[i, :, pl.ds(pl.multiple_of(t * half, half), half)], kgs[...])
            if i == 0:
                s1x[0, at, :] = total[:, :cols].astype(jnp.bfloat16)
                s1y[0, at, :] = total[:, cols:].astype(jnp.bfloat16)
            else:
                part[i, at, :] = total
            if i == 1:
                s1x[1, at, :] = total[:, :cols].astype(jnp.bfloat16)
            if i == 2:
                s1y[1, at, :] = total[:, cols:].astype(jnp.bfloat16)

        if i == 0:
            begin(RS1_X, s1x.at[0], r1x.at[0], xn)
            begin(RS1_Y, s1y.at[0], r1y.at[0], yn)
        if i == 1:
            begin(RS1_X + 1, s1x.at[1], r1x.at[1], xn)
        if i == 2:
            begin(RS1_Y + 1, s1y.at[1], r1y.at[1], yn)
    begin(OWN_X + 1, w.at[second], wall.at[d, second], xn)
    begin(OWN_Y + 1, w.at[second], wall.at[d, second], yn)

    def multiply(weights, block):
        @pl.loop(0, 2)
        def _(t):
            ig[:, columns(block, t * half, half)] = lax.dot_general(
                kg[...], weights[pl.ds(t * half, half), :], (((1,), (1,)), ((), ())), preferred_element_type=f32
            ).astype(jnp.bfloat16)

    multiply(w, d)
    copies[OWN_SIB].wait_recv()
    multiply(wall.at[sib], sib)

    copies[RS1_X].wait_recv()

    @pl.loop(0, 2)
    def _(t):
        at = pl.ds(t * half, half)
        s2y[at, :] = (part[2, at, :cols] + r1x[0, at, :].astype(f32)).astype(jnp.bfloat16)

    begin(RS2_Y, s2y, r2y, yn)
    copies[RS1_Y].wait_recv()

    @pl.loop(0, 2)
    def _(t):
        at = pl.ds(t * half, half)
        s2x[at, :] = (part[1, at, cols:] + r1y[0, at, :].astype(f32)).astype(jnp.bfloat16)

    begin(RS2_X, s2x, r2x, xn)
    copies[OWN_X].wait_recv()
    begin(FWD_Y, wall.at[xn, first], wall.at[xn, first], yn)
    copies[OWN_Y + 1].wait_recv()
    begin(FWD_X, wall.at[yn, second], wall.at[yn, second], xn)
    copies[OWN_X + 1].wait_recv()
    begin(SIB_X, wall.at[xn], wall.at[xn], sib)
    copies[OWN_Y].wait_recv()
    begin(SIB_Y, wall.at[yn], wall.at[yn], sib)
    multiply(wall.at[xn], xn)
    multiply(wall.at[yn], yn)
    copies[SIB_X].wait_recv()
    multiply(wall.at[sibling_of(xn)], sibling_of(xn))
    copies[SIB_Y].wait_recv()
    multiply(wall.at[sibling_of(yn)], sibling_of(yn))
    copies[RS1_X + 1].wait_recv()
    copies[RS1_Y + 1].wait_recv()
    copies[RS2_X].wait_recv()
    copies[RS2_Y].wait_recv()

    sums[0] = jnp.zeros_like(sums[0])

    @pl.loop(0, 8)
    def _(t):
        at = pl.ds(pl.multiple_of(t * (rows // 8), rows // 8), rows // 8)
        left = part[3, at, :cols] + r1x[1, at, :].astype(f32) + r2y[at, :].astype(f32)
        right = part[3, at, cols:] + r1y[1, at, :].astype(f32) + r2x[at, :].astype(f32)
        g[at, :cols] = left
        g[at, cols:] = right
        squared = left * left + right * right
        squares[at, :] = jnp.sum(squared, axis=1, keepdims=True)
        lanes = squared[:, :HD]
        for k in range(1, cols // HD):
            lanes += squared[:, k * HD : (k + 1) * HD]
        sums[0] += jnp.sum(lanes.reshape(rows // 64, 8, HD), axis=0)

    def sum_begin(stage):
        copy = pltpu.make_async_remote_copy(
            src_ref=sums.at[stage],
            dst_ref=got.at[stage],
            send_sem=sum_send.at[stage],
            recv_sem=sum_recv.at[stage],
            device_id=partners[stage],
            device_id_type=pl.DeviceIdType.MESH,
        )
        copies["sum", stage] = copy
        copy.start()

    def sum_end(stage):
        copies["sum", stage].wait_recv()
        sums[stage + 1] = sums[stage] + got[stage]

    last = len(partners) - 1
    for stage in range(last - 1):
        sum_begin(stage)
        sum_end(stage)
    sum_begin(last - 1)
    copies[FWD_X].wait_recv()
    copies[FWD_Y].wait_recv()
    begin(SIB_D, wall.at[dg], wall.at[dg], sib)
    sum_end(last - 1)
    sum_begin(last)
    multiply(wall.at[dg], dg)
    copies[SIB_D].wait_recv()
    multiply(wall.at[sibling_of(dg)], sibling_of(dg))
    sum_end(last)
    total = jnp.sum(jnp.sum(sums[last + 1], axis=0, keepdims=True), axis=1, keepdims=True)
    clip = jnp.minimum(1.0, 1.0 / jnp.sqrt(total + 1e-06))

    @pl.loop(0, 8)
    def _(t):
        at = pl.ds(pl.multiple_of(t * (rows // 8), rows // 8), rows // 8)
        fresh = state[at, :] + clip * clip * (squares[at, :] / w.shape[1])
        new_state[at, :] = fresh
        scale = learn_rate * clip / (jnp.sqrt(fresh) + 1e-10)
        new_w[at, :] = (w[at, :].astype(f32) - scale * g[at, :]).astype(jnp.bfloat16)

    for copy in copies.values():
        copy.wait_send()


def shards_cube(zs, hidden, key_weight, key_state, key_cotangent, doc_lengths):
    key_grad = rope_back(key_cotangent, positions_of(doc_lengths))
    tokens, width = hidden.shape
    rows, kvw = key_weight.shape
    cols = kvw // 2
    bf16, f32 = jnp.bfloat16, jnp.float32
    vmem = pl.BlockSpec(memory_space=pltpu.VMEM)
    stages = len(zs) + 3
    input_grad, new_weight, new_state = pl.pallas_call(
        functools.partial(exchange, zs),
        out_shape=(
            jax.ShapeDtypeStruct((tokens, width), bf16),
            jax.ShapeDtypeStruct((rows, kvw), bf16),
            jax.ShapeDtypeStruct((rows, 1), f32),
        ),
        in_specs=[vmem] * 4,
        out_specs=(vmem, vmem, vmem),
        scratch_shapes=[
            pltpu.VMEM((rows, kvw), f32),
            pltpu.VMEM((rows, 1), f32),
            pltpu.VMEM((stages + 1, 8, HD), f32),
            pltpu.VMEM((stages, 8, HD), f32),
            pltpu.VMEM((width // rows, rows, kvw), bf16),
            pltpu.VMEM((tokens, kvw), bf16),
            pltpu.VMEM((4, tokens, rows), bf16),
            pltpu.VMEM((4, rows, kvw), f32),
            pltpu.VMEM((2, rows, cols), bf16),
            pltpu.VMEM((2, rows, cols), bf16),
            pltpu.VMEM((2, rows, cols), bf16),
            pltpu.VMEM((2, rows, cols), bf16),
            pltpu.VMEM((rows, cols), bf16),
            pltpu.VMEM((rows, cols), bf16),
            pltpu.VMEM((rows, cols), bf16),
            pltpu.VMEM((rows, cols), bf16),
            pltpu.SemaphoreType.DMA((COPIES,)),
            pltpu.SemaphoreType.DMA((COPIES,)),
            pltpu.SemaphoreType.DMA((stages,)),
            pltpu.SemaphoreType.DMA((stages,)),
        ],
        compiler_params=pltpu.CompilerParams(
            collective_id=0, has_side_effects=True, vmem_limit_bytes=58 * 1024 * 1024
        ),
    )(key_grad, hidden, key_weight, key_state[:, None])
    return input_grad, new_weight, new_state[:, 0]


def solution(mesh):
    mp = mesh.shape["mp"]
    zs = tuple(2**k for k in range(mp.bit_length() - 1))
    cube = mesh.shape["dp"] == 2**3 and mp == 2 ** len(zs)
    return jax.shard_map(
        functools.partial(shards_cube, zs) if cube else shards,
        mesh=mesh,
        in_specs=(
            P("dp", "mp"),
            P(("mp", "dp"), None),
            P(("mp", "dp")),
            P("dp", None),
            P("dp", None),
        ),
        out_specs=(P("dp", "mp"), P(("mp", "dp"), None), P(("mp", "dp"))),
        check_vma=False,
    )
```

profile of v0, /device:TPU:0, one launch (start us, length us, event | category | flops | bytes accessed | tf_op | source)
XLA Modules:
  0.0 100.1 jit_solution(14040533197243685061)
XLA Ops:
  0.6 0.9 reduce_window_sum.11
  1.5 0.7 sub.21
  2.2 0.1 select_reduce_fusion
  2.3 1.5 %copy.9.state = f32[512,1]{1,0:T(8,128)} copy(f32[512,1]{0,1:T(1,128)} %bitcast.15) | data formatting | bytes 4096 | tf_op jit(solution)/shard_map/broadcast_in_dim | solution.py:322
  3.8 1.0 multiply_cosine_fusion
  4.8 1.5 %convert_bitcast_fusion = f32[64,8,8,128]{3,1,2,0:T(8,128)S(1)} fusion(bf16[512,1024]{1,0:T(8,128)(2,1)} %param.8), kind=kLoop, calls=%fused_computation | loop fusion | flops 524288 | bytes 3145728
  6.3 0.5 copy.10
  6.8 0.8 add_convert_fusion
  7.6 0.6 pad_maximum_fusion
  8.1 1.2 %copy.14 = bf16[64,8,8,128]{3,1,2,0:T(8,128)(2,1)} copy(bf16[64,8,8,128]{3,2,1,0:T(8,128)(2,1)S(1)} %bitcast.13) | data formatting | bytes 2097152
  9.4 83.3 %shard_map.76 = (bf16[512,4096]{1,0:T(8,128)(2,1)}, bf16[512,1024]{1,0:T(8,128)(2,1)}, f32[512,1]{1,0:T(8,128)}) custom-call(bf16[512,1024]{1,0:T(8,128)(2,1)} %bitcast.12, bf16[512,4096]{1,0:T(8,128)(2,1)} %hid.1, bf16[512,1024]{1,0:T(8,128)(2,1)} %w.1, f32[512,1]{1,0:T(8,128)} %copy.9.state), custom_call_target="tpu_custom_call" | custom-call | tf_op jit(solution)/shard_map/pallas_call | solution.py:288
  92.7 1.7 %reduce = f32[512]{0:T(512)} reduce(f32[512,1]{1,0:T(8,128)} %get-tuple-element.8, f32[]{:T(128)} %constant.15), dimensions={1}, to_apply=%get-tuple-element.8.reduce_sub_computation | reduce | bytes 4100 | tf_op jit(solution)/shard_map/pallas_call | solution.py:288
  94.4 0.0 copy-start
  94.4 4.8 %copy.17 = bf16[512,4096]{1,0:T(8,128)(2,1)} copy(bf16[512,4096]{1,0:T(8,128)(2,1)} %get-tuple-element.16) | data formatting | bytes 8388608
  99.2 0.0 copy-done
  99.2 1.0 copy.18
  (3 shorter events, 0.0 us)
Async XLA Ops:
  94.4 4.8 %copy-start = (bf16[512,1024]{1,0:T(8,128)(2,1)S(1)}, bf16[512,1024]{1,0:T(8,128)(2,1)}, u32[]{:S(2)}) copy-start(bf16[512,1024]{1,0:T(8,128)(2,1)} %get-tuple-element.17) | copy-start | bytes 3145732
where the time goes:
time: 100 us
  Pallas kernels  83.3 us (83%)
  local copies, waits for them, and re-layouts  9.02 us (9%)
  other arithmetic  7.14 us (7%)
    pallas_call x1, Pallas kernels, shards_cube(): pl.pallas_call(functools.partial(exchange, zs), out_shape=(jax.ShapeDtype...  83.3 us
    unnamed x7, local copies, waits for them, and re-layouts  7.48 us

commit v1 on v0

v1 whole, which is shorter than its diff:
```python
import functools

import jax
import jax.numpy as jnp
from jax import lax
from jax.experimental import pallas as pl
from jax.experimental.pallas import tpu as pltpu
from jax.sharding import PartitionSpec as P

HD = 128
LEN = 256


learn_rate = 0.01


def positions_of(doc_lengths):
    doc_ends = jnp.cumsum(doc_lengths, axis=1)
    doc_starts = doc_ends - doc_lengths
    places = jnp.arange(LEN, dtype=jnp.int32)
    before = doc_starts[:, None, :] <= places[None, :, None]
    doc_start = jnp.max(jnp.where(before, doc_starts[:, None, :], 0), axis=2)
    return (places[None, :] - doc_start).reshape(-1)


def rope_back(cotangent, positions):
    half_dim = HD // 2
    frequency = jnp.exp(
        -(2.0 * jnp.arange(half_dim, dtype=jnp.float32) / HD) * jnp.log(jnp.float32(500000.0))
    )
    angles = positions.astype(jnp.float32)[:, None] * frequency[None, :]
    cos_part = jnp.cos(angles)[:, None, :]
    sin_part = jnp.sin(angles)[:, None, :]
    gradients = cotangent.astype(jnp.float32).reshape(cotangent.shape[0], -1, HD)
    first_half = gradients[..., :half_dim]
    second_half = gradients[..., half_dim:]
    rotated = jnp.concatenate(
        [
            first_half * cos_part + second_half * sin_part,
            second_half * cos_part - first_half * sin_part,
        ],
        axis=-1,
    )
    return rotated.reshape(cotangent.shape[0], -1).astype(jnp.bfloat16)


def update(owned, key_weight, key_state):
    squared = owned * owned
    squares_sum = lax.psum(jnp.sum(squared), ("dp", "mp"))
    clip_factor = jnp.minimum(jnp.float32(1.0), 1.0 / jnp.sqrt(squares_sum + 1e-06))
    row_mean = jnp.mean(squared, axis=1)
    new_state = key_state + clip_factor * clip_factor * row_mean
    step_size = learn_rate * clip_factor * owned / (jnp.sqrt(new_state)[:, None] + 1e-10)
    new_weight = (key_weight.astype(jnp.float32) - step_size).astype(jnp.bfloat16)
    return new_weight, new_state


def shards(hidden, key_weight, key_state, key_cotangent, doc_lengths):
    positions = positions_of(doc_lengths)
    key_grad = rope_back(key_cotangent, positions)
    gathered = lax.dot_general(
        key_grad,
        lax.all_gather(key_weight, "dp", axis=0, tiled=True),
        (((1,), (1,)), ((), ())),
        preferred_element_type=jnp.float32,
    )
    input_grad = gathered.astype(jnp.bfloat16)
    owned = lax.psum_scatter(
        lax.dot_general(
            hidden, key_grad, (((0,), (0,)), ((), ())), preferred_element_type=jnp.float32
        ),
        "dp",
        scatter_dimension=0,
        tiled=True,
    )
    return (input_grad, *update(owned, key_weight, key_state))


COPIES = 64
LOCALS = 9


def exchange(zs, hid, w, state, cot, docs, freq, ig, new_w, new_state, wv, states, cots, lengths, freqs, hh, kga, part, s1x, s1y, r1x, r1y, s2x, s2y, r2x, r2y, wall, g, squares, square_rows, sums, got, local, send, recv, sum_send, sum_recv):
    f32, bf16 = jnp.float32, jnp.bfloat16
    rows, kvw = wv.shape
    tokens = cots.shape[0]
    half, step, cols = rows // 2, rows // 8, kvw // 2
    d = lax.axis_index("dp")
    core, xb, yb = lax.rem(d, 2), lax.rem(d // 2, 2), d // 4
    sib = d + 1 - 2 * core
    xn = d + 2 - 4 * xb
    yn = d + 4 - 8 * yb
    dg = xn + 4 - 8 * yb
    blocks = (dg, xn, yn, d)

    def sibling_of(block):
        return block + 1 - 2 * core

    def columns(block, at=0, size=None):
        size = rows if size is None else size
        return pl.ds(pl.multiple_of(block * rows + at, size), size)

    barrier = pltpu.get_barrier_semaphore()
    m = lax.axis_index("mp")
    partners = [{"dp": sib}]
    partners += [{"mp": m + bit - 2 * bit * lax.rem(m // bit, 2)} for bit in zs]
    partners += [{"dp": xn}, {"dp": yn}]
    for to in partners:
        pl.semaphore_signal(barrier, inc=1, device_id=to, device_id_type=pl.DeviceIdType.MESH)

    locals_ = []

    def fetch(src, dst):
        copy = pltpu.make_async_copy(src, dst, local.at[len(locals_)])
        locals_.append(copy)
        copy.start()
        return copy

    small = [fetch(docs, lengths), fetch(freq, freqs), fetch(cot, cots)]
    own_hid = [fetch(hid.at[:, columns(block)], hh.at[i, pl.ds(0, tokens)]) for i, block in enumerate(blocks)]
    own_w = fetch(w, wv)
    own_state = fetch(state, states)
    pl.semaphore_wait(barrier, len(partners))

    copies = {}

    def begin(name, src, dst, to):
        place = len(copies)
        copies[name] = pltpu.make_async_remote_copy(
            src_ref=src,
            dst_ref=dst,
            send_sem=send.at[place],
            recv_sem=recv.at[place],
            device_id={"dp": to},
            device_id_type=pl.DeviceIdType.MESH,
        )
        copies[name].start()

    first, second = pl.ds(0, half), pl.ds(half, half)
    begin("own_x", w.at[first], wall.at[d, first], xn)
    begin("own_y", w.at[second], wall.at[d, second], yn)
    for i, block in enumerate(blocks):
        begin(("hid", i), hid.at[:, columns(sibling_of(block))], hh.at[i, pl.ds(tokens, tokens)], sib)
    begin("own_sib", w, wall.at[d], sib)

    for copy in small:
        copy.wait()
    slab = LEN // 4
    for s in range(tokens // LEN):
        start, starts = jnp.int32(0), []
        for k in range(lengths.shape[1]):
            starts.append(start)
            start = start + lengths[s, k]

        @pl.loop(0, LEN // slab)
        def _(t, s=s, starts=starts):
            place = t * slab + lax.broadcasted_iota(jnp.int32, (slab, HD), 0)
            doc_start = jnp.zeros_like(place)
            for start in starts:
                doc_start = jnp.maximum(doc_start, jnp.where(start <= place, start, 0))
            angle = (place - doc_start).astype(f32) * freqs[...]
            cos_part = jnp.cos(angle)
            sin_part = jnp.sin(angle)
            lane = lax.broadcasted_iota(jnp.int32, (slab, HD), 1)
            sin_part = jnp.where(lane < HD // 2, sin_part, -sin_part)
            at = pl.ds(pl.multiple_of(s * LEN + t * slab, slab), slab)
            for h in range(kvw // HD):
                head = pl.ds(h * HD, HD)
                value = cots[at, head].astype(f32)
                kga[at, head] = (value * cos_part + pltpu.roll(value, HD // 2, 1) * sin_part).astype(bf16)

    mine = pl.ds(0, tokens)
    begin("kg", kga.at[mine], kga.at[pl.ds(tokens, tokens)], sib)
    for copy in own_hid:
        copy.wait()
    own_w.wait()
    own_state.wait()

    def multiply(weights, block, at=0, size=rows, tile=half):
        tile = min(tile, size)

        @pl.loop(0, size // tile)
        def _(t):
            ig[:, columns(block, at + t * tile, tile)] = lax.dot_general(
                kga[mine, :], weights[pl.ds(pl.multiple_of(at + t * tile, tile), tile), :], (((1,), (1,)), ((), ())), preferred_element_type=f32
            ).astype(bf16)

    copies["kg"].wait_recv()
    for i in range(4):
        copies["hid", i].wait_recv()

        @pl.loop(0, 2)
        def _(t, i=i):
            at = pl.ds(pl.multiple_of(t * half, half), half)
            total = lax.dot_general(hh[i, :, at], kga[...], (((0,), (0,)), ((), ())), preferred_element_type=f32)
            if i == 0:
                s1x[0, at, :] = total[:, :cols].astype(bf16)
                s1y[0, at, :] = total[:, cols:].astype(bf16)
            if i == 1:
                s1x[1, at, :] = total[:, :cols].astype(bf16)
                part[0, at, :] = total[:, cols:]
            if i == 2:
                s1y[1, at, :] = total[:, cols:].astype(bf16)
                part[1, at, :] = total[:, :cols]
            if i == 3:
                part[2, at, :] = total[:, :cols]
                part[3, at, :] = total[:, cols:]

        if i == 0:
            begin(("rs1_x", 0), s1x.at[0], r1x.at[0], xn)
            begin(("rs1_y", 0), s1y.at[0], r1y.at[0], yn)
        if i == 1:
            begin(("rs1_x", 1), s1x.at[1], r1x.at[1], xn)
        if i == 2:
            begin(("rs1_y", 1), s1y.at[1], r1y.at[1], yn)

    multiply(wv, d)
    copies["own_sib"].wait_recv()
    multiply(wall.at[sib], sib)
    copies["own_x"].wait_recv()
    begin("sib_x", wall.at[xn, first], wall.at[xn, first], sib)
    copies["own_y"].wait_recv()
    begin("sib_y", wall.at[yn, second], wall.at[yn, second], sib)
    multiply(wall.at[xn], xn, 0, half)
    multiply(wall.at[yn], yn, half, half)

    copies["rs1_x", 0].wait_recv()

    @pl.loop(0, 4)
    def _(t):
        at = pl.ds(pl.multiple_of(t * (rows // 4), rows // 4), rows // 4)
        s2y[at, :] = (part[1, at, :] + r1x[0, at, :].astype(f32)).astype(bf16)

    begin("rs2_y", s2y, r2y, yn)
    copies["rs1_y", 0].wait_recv()

    @pl.loop(0, 4)
    def _(t):
        at = pl.ds(pl.multiple_of(t * (rows // 4), rows // 4), rows // 4)
        s2x[at, :] = (part[0, at, :] + r1y[0, at, :].astype(f32)).astype(bf16)

    begin("rs2_x", s2x, r2x, xn)

    def forward(k):
        low, high = pl.ds(k * step, step), pl.ds(half + k * step, step)
        begin(("fwd_x", k), wall.at[yn, high], wall.at[yn, high], xn)
        begin(("fwd_y", k), wall.at[xn, low], wall.at[xn, low], yn)

    def late(k):
        low, high = pl.ds(k * step, step), pl.ds(half + k * step, step)
        begin(("late_x", k), wv.at[high], wall.at[d, high], xn)
        begin(("late_y", k), wv.at[low], wall.at[d, low], yn)

    def pass_forward(k):
        low, high = pl.ds(k * step, step), pl.ds(half + k * step, step)
        copies["fwd_x", k].wait_recv()
        begin(("sib_fx", k), wall.at[dg, high], wall.at[dg, high], sib)
        copies["fwd_y", k].wait_recv()
        begin(("sib_fy", k), wall.at[dg, low], wall.at[dg, low], sib)

    def pass_late(k):
        low, high = pl.ds(k * step, step), pl.ds(half + k * step, step)
        copies["late_x", k].wait_recv()
        begin(("sib_lx", k), wall.at[xn, high], wall.at[xn, high], sib)
        copies["late_y", k].wait_recv()
        begin(("sib_ly", k), wall.at[yn, low], wall.at[yn, low], sib)

    for k in range(3):
        forward(k)
    copies["sib_x"].wait_recv()
    copies["sib_y"].wait_recv()
    multiply(wall.at[sibling_of(xn)], sibling_of(xn), 0, half)
    multiply(wall.at[sibling_of(yn)], sibling_of(yn), half, half)

    copies["rs1_x", 1].wait_recv()
    copies["rs1_y", 1].wait_recv()
    copies["rs2_x"].wait_recv()
    copies["rs2_y"].wait_recv()

    sums[0] = jnp.zeros_like(sums[0])
    for t in range(rows // HD):
        at = pl.ds(t * HD, HD)
        left = part[2, at, :] + r1x[1, at, :].astype(f32) + r2y[at, :].astype(f32)
        right = part[3, at, :] + r1y[1, at, :].astype(f32) + r2x[at, :].astype(f32)
        g[at, :cols] = left
        g[at, cols:] = right
        squared = left * left + right * right
        lanes = squared[:, :HD]
        for k in range(1, cols // HD):
            lanes += squared[:, k * HD : (k + 1) * HD]
        squares[at, :] = jnp.sum(lanes, axis=1, keepdims=True)
        square_rows[pl.ds(t, 1), :] = jnp.sum(lanes.T, axis=0, keepdims=True)
        sums[0] += jnp.sum(lanes.reshape(HD // 8, 8, HD), axis=0)

    def sum_begin(stage):
        copy = pltpu.make_async_remote_copy(
            src_ref=sums.at[stage],
            dst_ref=got.at[stage],
            send_sem=sum_send.at[stage],
            recv_sem=sum_recv.at[stage],
            device_id=partners[stage],
            device_id_type=pl.DeviceIdType.MESH,
        )
        copies["sum", stage] = copy
        copy.start()

    def sum_end(stage):
        copies["sum", stage].wait_recv()
        sums[stage + 1] = sums[stage] + got[stage]

    last = len(partners) - 1
    for stage in range(last - 1):
        sum_begin(stage)
        if stage == 0:
            pass_forward(0)
        sum_end(stage)
    sum_begin(last - 1)
    forward(3)
    late(0)
    pass_forward(1)
    sum_end(last - 1)
    sum_begin(last)
    for k in range(1, 4):
        late(k)
    multiply(wall.at[dg], dg, 0, 2 * step)
    multiply(wall.at[dg], dg, half, 2 * step)
    sum_end(last)
    total = jnp.sum(jnp.sum(sums[last + 1], axis=0, keepdims=True), axis=1, keepdims=True)
    clip = jnp.minimum(1.0, 1.0 / jnp.sqrt(total + 1e-06))

    for t in range(rows // HD):
        at = pl.ds(t * HD, HD)
        state_row = states[pl.ds(t, 1), :]
        new_state[pl.ds(t, 1), :] = state_row + clip * clip * (square_rows[pl.ds(t, 1), :] / kvw)
        old = jnp.broadcast_to(state_row, (HD, HD)).T
        fresh = old + clip * clip * (squares[at, :] / kvw)
        scale = learn_rate * clip / (jnp.sqrt(fresh) + 1e-10)
        for k in range(kvw // HD):
            lanes_at = pl.ds(k * HD, HD)
            new_w[at, lanes_at] = (wv[at, lanes_at].astype(f32) - scale * g[at, lanes_at]).astype(bf16)

    pass_forward(2)
    pass_forward(3)
    multiply(wall.at[dg], dg, 2 * step, 2 * step)
    multiply(wall.at[dg], dg, half + 2 * step, 2 * step)
    for k in range(4):
        copies["sib_fx", k].wait_recv()
        copies["sib_fy", k].wait_recv()
    multiply(wall.at[sibling_of(dg)], sibling_of(dg))
    for pair in range(2):
        for k in (2 * pair, 2 * pair + 1):
            pass_late(k)
        at = 2 * pair * step
        multiply(wall.at[xn], xn, half + at, 2 * step)
        multiply(wall.at[yn], yn, at, 2 * step)
        for k in (2 * pair, 2 * pair + 1):
            copies["sib_lx", k].wait_recv()
            copies["sib_ly", k].wait_recv()
        multiply(wall.at[sibling_of(xn)], sibling_of(xn), half + at, 2 * step)
        multiply(wall.at[sibling_of(yn)], sibling_of(yn), at, 2 * step)

    for copy in copies.values():
        copy.wait_send()


def shards_cube(zs, hidden, key_weight, key_state, key_cotangent, doc_lengths):
    tokens, width = hidden.shape
    rows, kvw = key_weight.shape
    cols = kvw // 2
    bf16, f32 = jnp.bfloat16, jnp.float32
    half_dim = HD // 2
    frequency = jnp.exp(
        -(2.0 * jnp.arange(half_dim, dtype=jnp.float32) / HD) * jnp.log(jnp.float32(500000.0))
    )
    frequency = jnp.concatenate([frequency, frequency])[None, :]
    held = pl.BlockSpec(memory_space=pl.ANY)
    vmem = pl.BlockSpec(memory_space=pltpu.VMEM)
    stages = len(zs) + 3
    groups = rows // HD
    input_grad, new_weight, new_state = pl.pallas_call(
        functools.partial(exchange, zs),
        out_shape=(
            pltpu.VMEM((tokens, width), bf16),
            pltpu.VMEM((rows, kvw), bf16),
            pltpu.VMEM((groups, HD), f32),
        ),
        in_specs=[held] * 6,
        out_specs=(vmem, vmem, vmem),
        scratch_shapes=[
            pltpu.VMEM((rows, kvw), bf16),
            pltpu.VMEM((groups, HD), f32),
            pltpu.VMEM((tokens, kvw), bf16),
            pltpu.SMEM(doc_lengths.shape, jnp.int32),
            pltpu.VMEM((1, HD), f32),
            pltpu.VMEM((4, 2 * tokens, rows), bf16),
            pltpu.VMEM((2 * tokens, kvw), bf16),
            pltpu.VMEM((4, rows, cols), f32),
            pltpu.VMEM((2, rows, cols), bf16),
            pltpu.VMEM((2, rows, cols), bf16),
            pltpu.VMEM((2, rows, cols), bf16),
            pltpu.VMEM((2, rows, cols), bf16),
            pltpu.VMEM((rows, cols), bf16),
            pltpu.VMEM((rows, cols), bf16),
            pltpu.VMEM((rows, cols), bf16),
            pltpu.VMEM((rows, cols), bf16),
            pltpu.VMEM((width // rows, rows, kvw), bf16),
            pltpu.VMEM((rows, kvw), f32),
            pltpu.VMEM((rows, 1), f32),
            pltpu.VMEM((groups, HD), f32),
            pltpu.VMEM((stages + 1, 8, HD), f32),
            pltpu.VMEM((stages, 8, HD), f32),
            pltpu.SemaphoreType.DMA((LOCALS,)),
            pltpu.SemaphoreType.DMA((COPIES,)),
            pltpu.SemaphoreType.DMA((COPIES,)),
            pltpu.SemaphoreType.DMA((stages,)),
            pltpu.SemaphoreType.DMA((stages,)),
        ],
        compiler_params=pltpu.CompilerParams(
            collective_id=0, has_side_effects=True, vmem_limit_bytes=56 * 1024 * 1024
        ),
    )(hidden, key_weight, key_state.reshape(groups, HD), key_cotangent, doc_lengths, frequency)
    return input_grad, new_weight, new_state.reshape(rows)


def solution(mesh):
    mp = mesh.shape["mp"]
    zs = tuple(2**k for k in range(mp.bit_length() - 1))
    cube = mesh.shape["dp"] == 2**3 and mp == 2 ** len(zs)
    return jax.shard_map(
        functools.partial(shards_cube, zs) if cube else shards,
        mesh=mesh,
        in_specs=(
            P("dp", "mp"),
            P(("mp", "dp"), None),
            P(("mp", "dp")),
            P("dp", None),
            P("dp", None),
        ),
        out_specs=(P("dp", "mp"), P(("mp", "dp"), None), P(("mp", "dp"))),
        check_vma=False,
    )
```

time: 100 us -> 83.2 us (0.83)
  other arithmetic: 7.14 us -> 0.6 us
  Pallas kernels: 83.3 us -> 77.6 us
  local copies, waits for them, and re-layouts: 9.02 us -> 3.56 us
    pallas_call x1, Pallas kernels: 83.3 us -> 77.6 us  [shards_cube(): pl.pallas_call(functools.partial(exchange, zs), out_shape=(pltpu.VMEM((to...]
    unnamed x7 -> x3, local copies, waits for them, and re-layouts: 7.48 us -> 3.56 us
    pallas_call x1 -> x0, other arithmetic: 1.68 us -> none  [shards_cube(): pl.pallas_call(functools.partial(exchange, zs), out_shape=(jax.ShapeDtype...]
    another operation x2 -> x0, other arithmetic: 1.64 us -> none  [the longest x1 0.85 us: positions_of(): doc_ends = jnp.cumsum(doc_lengths, axis=1)]
    broadcast_in_dim x1 -> x0, local copies, waits for them, and re-layouts: 1.54 us -> none  [shards_cube(): key_state[:, None]]
    unnamed x2 -> x0, other arithmetic: 1.48 us -> none
where the time goes in v1:
time: 83.2 us; the launch traced here: 82.4 us
  Pallas kernels  77.6 us (93%)
  local copies, waits for them, and re-layouts  3.56 us (4%)
    pallas_call x1, Pallas kernels, shards_cube(): pl.pallas_call(functools.partial(exchange, zs), out_shape=(pltpu.VMEM((to...  77.6 us
    unnamed x3, local copies, waits for them, and re-layouts  3.56 us

profile of v1, /device:TPU:0, one launch (start us, length us, event | category | flops | bytes accessed | tf_op | source)
XLA Modules:
  0.0 82.4 jit_solution(6577908907146791748)
XLA Ops:
  0.6 0.6 maximum_bitcast_fusion.freq
  1.2 77.6 %shard_map.76 = (bf16[512,4096]{1,0:T(8,128)(2,1)S(1)}, bf16[512,1024]{1,0:T(8,128)(2,1)S(1)}, f32[4,128]{1,0:T(4,128)S(1)}) custom-call(bf16[512,4096]{1,0:T(8,128)(2,1)} %hid.1, bf16[512,1024]{1,0:T(8,128)(2,1)} %w.1, f32[4,128]{1,0:T(4,128)} %bitcast.5, bf16[512,1024]{1,0:T(8,128)(2,1)} %cot.1, s32[2,4]{1,0:T(2,128)} %docs.1, ...), custom_call_target="tpu_custom_call" | custom-call | tf_op jit(solution)/shard_map/pallas_call | solution.py:380
  78.8 2.0 %copy.11 = bf16[512,4096]{1,0:T(8,128)(2,1)} copy(bf16[512,4096]{1,0:T(8,128)(2,1)S(1)} %get-tuple-element.9) | data formatting | bytes 8388608
  80.8 0.6 copy.13
  81.4 1.0 %copy.12 = bf16[512,1024]{1,0:T(8,128)(2,1)} copy(bf16[512,1024]{1,0:T(8,128)(2,1)S(1)} %get-tuple-element.10) | data formatting | bytes 2097152
  (1 shorter events, 0.0 us)

commit v2 on v1

--- a/solution.py
+++ b/solution.py
@@ -77,10 +77,10 @@
 
 
 COPIES = 64
-LOCALS = 9
-
-
-def exchange(zs, hid, w, state, cot, docs, freq, ig, new_w, new_state, wv, states, cots, lengths, freqs, hh, kga, part, s1x, s1y, r1x, r1y, s2x, s2y, r2x, r2y, wall, g, squares, square_rows, sums, got, local, send, recv, sum_send, sum_recv):
+LOCALS = 8
+
+
+def exchange(zs, hid, w, state, cot, docs, ig, new_w, new_state, kg, tails, wv, states, cots, lengths, hh, kga, part, s1x, s1y, r1x, r1y, s2x, s2y, r2x, r2y, wall, g, squares, square_rows, sums, got, local, ready, send, recv, sum_send, sum_recv):
     f32, bf16 = jnp.float32, jnp.bfloat16
     rows, kvw = wv.shape
     tokens = cots.shape[0]
@@ -105,8 +105,23 @@
     partners = [{"dp": sib}]
     partners += [{"mp": m + bit - 2 * bit * lax.rem(m // bit, 2)} for bit in zs]
     partners += [{"dp": xn}, {"dp": yn}]
-    for to in partners:
-        pl.semaphore_signal(barrier, inc=1, device_id=to, device_id_type=pl.DeviceIdType.MESH)
+    late_half = [core] + [lax.rem(m // bit, 2) for bit in zs]
+
+    def signal(semaphore, to):
+        pl.semaphore_signal(semaphore, inc=1, device_id=to, device_id_type=pl.DeviceIdType.MESH)
+
+    for to in partners[-2:]:
+        signal(barrier, to)
+    for j, upper in enumerate(late_half):
+
+        @pl.when(upper == 0)
+        def _(j=j):
+            signal(barrier, partners[j])
+
+    def greeted(j):
+        @pl.when(late_half[j] == 0)
+        def _():
+            pl.semaphore_wait(ready.at[j], 1)
 
     locals_ = []
 
@@ -116,11 +131,11 @@
         copy.start()
         return copy
 
-    small = [fetch(docs, lengths), fetch(freq, freqs), fetch(cot, cots)]
+    small = [fetch(docs, lengths), fetch(cot, cots)]
     own_hid = [fetch(hid.at[:, columns(block)], hh.at[i, pl.ds(0, tokens)]) for i, block in enumerate(blocks)]
     own_w = fetch(w, wv)
     own_state = fetch(state, states)
-    pl.semaphore_wait(barrier, len(partners))
+    pl.semaphore_wait(barrier, 2 + sum(late_half))
 
     copies = {}
 
@@ -139,6 +154,13 @@
     first, second = pl.ds(0, half), pl.ds(half, half)
     begin("own_x", w.at[first], wall.at[d, first], xn)
     begin("own_y", w.at[second], wall.at[d, second], yn)
+    for j, upper in enumerate(late_half):
+
+        @pl.when(upper == 1)
+        def _(j=j):
+            signal(ready.at[j], partners[j])
+
+    greeted(0)
     for i, block in enumerate(blocks):
         begin(("hid", i), hid.at[:, columns(sibling_of(block))], hh.at[i, pl.ds(tokens, tokens)], sib)
     begin("own_sib", w, wall.at[d], sib)
@@ -146,6 +168,8 @@
     for copy in small:
         copy.wait()
     slab = LEN // 4
+    pair = lax.rem(lax.broadcasted_iota(jnp.int32, (1, HD), 1), HD // 2).astype(f32)
+    frequency = jnp.exp(-(2.0 * pair / HD) * jnp.log(jnp.float32(500000.0)))
     for s in range(tokens // LEN):
         start, starts = jnp.int32(0), []
         for k in range(lengths.shape[1]):
@@ -158,7 +182,7 @@
             doc_start = jnp.zeros_like(place)
             for start in starts:
                 doc_start = jnp.maximum(doc_start, jnp.where(start <= place, start, 0))
-            angle = (place - doc_start).astype(f32) * freqs[...]
+            angle = (place - doc_start).astype(f32) * frequency
             cos_part = jnp.cos(angle)
             sin_part = jnp.sin(angle)
             lane = lax.broadcasted_iota(jnp.int32, (slab, HD), 1)
@@ -167,7 +191,9 @@
             for h in range(kvw // HD):
                 head = pl.ds(h * HD, HD)
                 value = cots[at, head].astype(f32)
-                kga[at, head] = (value * cos_part + pltpu.roll(value, HD // 2, 1) * sin_part).astype(bf16)
+                turned = (value * cos_part + pltpu.roll(value, HD // 2, 1) * sin_part).astype(bf16)
+                kga[at, head] = turned
+                kg[at, head] = turned
 
     mine = pl.ds(0, tokens)
     begin("kg", kga.at[mine], kga.at[pl.ds(tokens, tokens)], sib)
@@ -248,8 +274,11 @@
 
     def late(k):
         low, high = pl.ds(k * step, step), pl.ds(half + k * step, step)
-        begin(("late_x", k), wv.at[high], wall.at[d, high], xn)
-        begin(("late_y", k), wv.at[low], wall.at[d, low], yn)
+        to_x, to_y = wall.at[d, high], wall.at[d, low]
+        if k >= 2:
+            to_x, to_y = (tails.at[i, pl.ds((k - 2) * step, step)] for i in range(2))
+        begin(("late_x", k), wv.at[high], to_x, xn)
+        begin(("late_y", k), wv.at[low], to_y, yn)
 
     def pass_forward(k):
         low, high = pl.ds(k * step, step), pl.ds(half + k * step, step)
@@ -260,12 +289,19 @@
 
     def pass_late(k):
         low, high = pl.ds(k * step, step), pl.ds(half + k * step, step)
+        at = pl.ds((k - 2) * step, step)
         copies["late_x", k].wait_recv()
-        begin(("sib_lx", k), wall.at[xn, high], wall.at[xn, high], sib)
+        if k < 2:
+            begin(("sib_lx", k), wall.at[xn, high], wall.at[xn, high], sib)
+        else:
+            begin(("sib_lx", k), tails.at[0, at], tails.at[2, at], sib)
         copies["late_y", k].wait_recv()
-        begin(("sib_ly", k), wall.at[yn, low], wall.at[yn, low], sib)
-
-    for k in range(3):
+        if k < 2:
+            begin(("sib_ly", k), wall.at[yn, low], wall.at[yn, low], sib)
+        else:
+            begin(("sib_ly", k), tails.at[1, at], tails.at[3, at], sib)
+
+    for k in range(4):
         forward(k)
     copies["sib_x"].wait_recv()
     copies["sib_y"].wait_recv()
@@ -310,17 +346,19 @@
 
     last = len(partners) - 1
     for stage in range(last - 1):
+        if stage:
+            greeted(stage)
         sum_begin(stage)
         if stage == 0:
             pass_forward(0)
         sum_end(stage)
     sum_begin(last - 1)
-    forward(3)
     late(0)
+    late(1)
     pass_forward(1)
     sum_end(last - 1)
     sum_begin(last)
-    for k in range(1, 4):
+    for k in range(2, 4):
         late(k)
     multiply(wall.at[dg], dg, 0, 2 * step)
     multiply(wall.at[dg], dg, half, 2 * step)
@@ -347,20 +385,63 @@
         copies["sib_fx", k].wait_recv()
         copies["sib_fy", k].wait_recv()
     multiply(wall.at[sibling_of(dg)], sibling_of(dg))
-    for pair in range(2):
-        for k in (2 * pair, 2 * pair + 1):
-            pass_late(k)
-        at = 2 * pair * step
-        multiply(wall.at[xn], xn, half + at, 2 * step)
-        multiply(wall.at[yn], yn, at, 2 * step)
-        for k in (2 * pair, 2 * pair + 1):
-            copies["sib_lx", k].wait_recv()
-            copies["sib_ly", k].wait_recv()
-        multiply(wall.at[sibling_of(xn)], sibling_of(xn), half + at, 2 * step)
-        multiply(wall.at[sibling_of(yn)], sibling_of(yn), at, 2 * step)
+    for k in range(2):
+        pass_late(k)
+    multiply(wall.at[xn], xn, half, 2 * step)
+    multiply(wall.at[yn], yn, 0, 2 * step)
+    for k in range(2):
+        copies["sib_lx", k].wait_recv()
+        copies["sib_ly", k].wait_recv()
+    multiply(wall.at[sibling_of(xn)], sibling_of(xn), half, 2 * step)
+    multiply(wall.at[sibling_of(yn)], sibling_of(yn), 0, 2 * step)
+    for k in range(2, 4):
+        pass_late(k)
+    for k in range(2, 4):
+        copies["sib_lx", k].wait_recv()
+        copies["sib_ly", k].wait_recv()
 
     for copy in copies.values():
         copy.wait_send()
+
+
+def finish(ig_part, kg, tails, w_part, state_part, ig, new_w, new_state, last, sems):
+    rows = w_part.shape[0]
+    half, tail = rows // 2, tails.shape[1]
+    d = lax.axis_index("dp")
+    core, xb, yb = lax.rem(d, 2), lax.rem(d // 2, 2), d // 4
+    xn = d + 2 - 4 * xb
+    yn = d + 4 - 8 * yb
+    dg = xn + 4 - 8 * yb
+    flip = 1 - 2 * core
+    copies = []
+
+    def put(src, dst):
+        copy = pltpu.make_async_copy(src, dst, sems.at[len(copies)])
+        copies.append(copy)
+        copy.start()
+
+    def ready(block, at, size):
+        where = pl.ds(pl.multiple_of(block * rows + at, HD), size)
+        put(ig_part.at[:, where], ig.at[:, where])
+
+    for block in (d, dg):
+        for owner in (block, block + flip):
+            ready(owner, 0, rows)
+    for owner in (xn, xn + flip):
+        ready(owner, 0, rows - tail)
+    for owner in (yn, yn + flip):
+        ready(owner, 0, half - tail)
+        ready(owner, half, half)
+    put(w_part, new_w)
+    put(state_part, new_state)
+    for i, owner in enumerate((xn, yn, xn + flip, yn + flip)):
+        last[i] = lax.dot_general(
+            kg[...], tails[i], (((1,), (1,)), ((), ())), preferred_element_type=jnp.float32
+        ).astype(jnp.bfloat16)
+        at = (half if i % 2 else rows) - tail
+        put(last.at[i], ig.at[:, pl.ds(pl.multiple_of(owner * rows + at, HD), tail)])
+    for copy in copies:
+        copy.wait()
 
 
 def shards_cube(zs, hidden, key_weight, key_state, key_cotangent, doc_lengths):
@@ -368,30 +449,27 @@
     rows, kvw = key_weight.shape
     cols = kvw // 2
     bf16, f32 = jnp.bfloat16, jnp.float32
-    half_dim = HD // 2
-    frequency = jnp.exp(
-        -(2.0 * jnp.arange(half_dim, dtype=jnp.float32) / HD) * jnp.log(jnp.float32(500000.0))
-    )
-    frequency = jnp.concatenate([frequency, frequency])[None, :]
     held = pl.BlockSpec(memory_space=pl.ANY)
     vmem = pl.BlockSpec(memory_space=pltpu.VMEM)
     stages = len(zs) + 3
     groups = rows // HD
-    input_grad, new_weight, new_state = pl.pallas_call(
+    tail = rows // 4
+    *parts, kg, tails = pl.pallas_call(
         functools.partial(exchange, zs),
         out_shape=(
             pltpu.VMEM((tokens, width), bf16),
             pltpu.VMEM((rows, kvw), bf16),
             pltpu.VMEM((groups, HD), f32),
+            pltpu.VMEM((tokens, kvw), bf16),
+            pltpu.VMEM((4, tail, kvw), bf16),
         ),
-        in_specs=[held] * 6,
-        out_specs=(vmem, vmem, vmem),
+        in_specs=[held] * 5,
+        out_specs=(vmem,) * 5,
         scratch_shapes=[
             pltpu.VMEM((rows, kvw), bf16),
             pltpu.VMEM((groups, HD), f32),
             pltpu.VMEM((tokens, kvw), bf16),
             pltpu.SMEM(doc_lengths.shape, jnp.int32),
-            pltpu.VMEM((1, HD), f32),
             pltpu.VMEM((4, 2 * tokens, rows), bf16),
             pltpu.VMEM((2 * tokens, kvw), bf16),
             pltpu.VMEM((4, rows, cols), f32),
@@ -410,6 +488,7 @@
             pltpu.VMEM((stages + 1, 8, HD), f32),
             pltpu.VMEM((stages, 8, HD), f32),
             pltpu.SemaphoreType.DMA((LOCALS,)),
+            pltpu.SemaphoreType.REGULAR((1 + len(zs),)),
             pltpu.SemaphoreType.DMA((COPIES,)),
             pltpu.SemaphoreType.DMA((COPIES,)),
             pltpu.SemaphoreType.DMA((stages,)),
@@ -418,7 +497,19 @@
         compiler_params=pltpu.CompilerParams(
             collective_id=0, has_side_effects=True, vmem_limit_bytes=56 * 1024 * 1024
         ),
-    )(hidden, key_weight, key_state.reshape(groups, HD), key_cotangent, doc_lengths, frequency)
+    )(hidden, key_weight, key_state.reshape(groups, HD), key_cotangent, doc_lengths)
+    input_grad, new_weight, new_state = pl.pallas_call(
+        finish,
+        out_shape=(
+            jax.ShapeDtypeStruct((tokens, width), bf16),
+            jax.ShapeDtypeStruct((rows, kvw), bf16),
+            jax.ShapeDtypeStruct((groups, HD), f32),
+        ),
+        in_specs=[held, vmem, vmem, held, held],
+        out_specs=(held,) * 3,
+        scratch_shapes=[pltpu.VMEM((4, tokens, tail), bf16), pltpu.SemaphoreType.DMA((16,))],
+        compiler_params=pltpu.CompilerParams(vmem_limit_bytes=4 * 1024 * 1024),
+    )(parts[0], kg, tails, *parts[1:])
     return input_grad, new_weight, new_state.reshape(rows)
 
 

time: 83.2 us -> 80.9 us (0.972)
  local copies, waits for them, and re-layouts: 3.56 us -> 0 us
  Pallas kernels: 77.6 us -> 80.1 us
    unnamed x3 -> x0, local copies, waits for them, and re-layouts: 3.56 us -> none
    pallas_call x0 -> x1, Pallas kernels: none -> 2.49 us  [shards_cube(): pl.pallas_call(finish, out_shape=(jax.ShapeDtypeStruct((tokens, width), b...]
where the time goes in v2:
time: 80.9 us; the launch traced here: 80.7 us
  Pallas kernels  80.1 us (99%)
    pallas_call x1, Pallas kernels, shards_cube(): pl.pallas_call(functools.partial(exchange, zs), out_shape=(pltpu.VMEM((to...  77.6 us
    pallas_call x1, Pallas kernels, shards_cube(): pl.pallas_call(finish, out_shape=(jax.ShapeDtypeStruct((tokens, width), b...  2.49 us

profile of v2, /device:TPU:0, one launch (start us, length us, event | category | flops | bytes accessed | tf_op | source)
XLA Modules:
  0.0 80.7 jit_solution(8909129700681259457)
XLA Ops:
  0.6 77.6 %shard_map.76 = (bf16[512,4096]{1,0:T(8,128)(2,1)S(1)}, bf16[512,1024]{1,0:T(8,128)(2,1)S(1)}, f32[4,128]{1,0:T(4,128)S(1)}, bf16[512,1024]{1,0:T(8,128)(2,1)S(1)}, bf16[4,128,1024]{2,1,0:T(8,128)(2,1)S(1)}) custom-call(bf16[512,4096]{1,0:T(8,128)(2,1)} %hid.1, bf16[512,1024]{1,0:T(8,128)(2,1)} %w.1, f32[4,128]{1,0:T(4,128)} %bitcast.2, ...), custom_call_target="tpu_custom_call" | custom-call | tf_op jit(solution)/shard_map/pallas_call | solution.py:457
  78.2 2.5 %shard_map.77 = (bf16[512,4096]{1,0:T(8,128)(2,1)}, bf16[512,1024]{1,0:T(8,128)(2,1)}, f32[4,128]{1,0:T(4,128)}) custom-call(bf16[512,4096]{1,0:T(8,128)(2,1)S(1)} %get-tuple-element.11.ig_part, bf16[512,1024]{1,0:T(8,128)(2,1)S(1)} %get-tuple-element.12.kg, bf16[4,128,1024]{2,1,0:T(8,128)(2,1)S(1)} %get-tuple-element.13.tails, ...), custom_call_target="tpu_custom_call" | custom-call | tf_op jit(solution)/shard_map/pallas_call | solution.py:501

commit v3 on v2

--- a/solution.py
+++ b/solution.py
@@ -102,17 +102,16 @@
 
     barrier = pltpu.get_barrier_semaphore()
     m = lax.axis_index("mp")
-    partners = [{"dp": sib}]
+    partners = [{"dp": sib}, {"dp": xn}, {"dp": yn}]
     partners += [{"mp": m + bit - 2 * bit * lax.rem(m // bit, 2)} for bit in zs]
-    partners += [{"dp": xn}, {"dp": yn}]
-    late_half = [core] + [lax.rem(m // bit, 2) for bit in zs]
+    late_half = {0: core, **{3 + j: lax.rem(m // bit, 2) for j, bit in enumerate(zs)}}
 
     def signal(semaphore, to):
         pl.semaphore_signal(semaphore, inc=1, device_id=to, device_id_type=pl.DeviceIdType.MESH)
 
-    for to in partners[-2:]:
+    for to in partners[1:3]:
         signal(barrier, to)
-    for j, upper in enumerate(late_half):
+    for j, upper in late_half.items():
 
         @pl.when(upper == 0)
         def _(j=j):
@@ -135,7 +134,7 @@
     own_hid = [fetch(hid.at[:, columns(block)], hh.at[i, pl.ds(0, tokens)]) for i, block in enumerate(blocks)]
     own_w = fetch(w, wv)
     own_state = fetch(state, states)
-    pl.semaphore_wait(barrier, 2 + sum(late_half))
+    pl.semaphore_wait(barrier, 2 + sum(late_half.values()))
 
     copies = {}
 
@@ -154,7 +153,7 @@
     first, second = pl.ds(0, half), pl.ds(half, half)
     begin("own_x", w.at[first], wall.at[d, first], xn)
     begin("own_y", w.at[second], wall.at[d, second], yn)
-    for j, upper in enumerate(late_half):
+    for j, upper in late_half.items():
 
         @pl.when(upper == 1)
         def _(j=j):
@@ -301,7 +300,7 @@
         else:
             begin(("sib_ly", k), tails.at[1, at], tails.at[3, at], sib)
 
-    for k in range(4):
+    for k in range(2):
         forward(k)
     copies["sib_x"].wait_recv()
     copies["sib_y"].wait_recv()
@@ -344,25 +343,38 @@
         copies["sum", stage].wait_recv()
         sums[stage + 1] = sums[stage] + got[stage]
 
+    def quarters(block, at):
+        multiply(wall.at[block], block, at, 2 * step)
+        multiply(wall.at[block], block, half + at, 2 * step)
+
+    def from_sibling(names):
+        for name in names:
+            copies[name].wait_recv()
+
+    sum_begin(0)
+    pass_forward(0)
+    sum_end(0)
+    sum_begin(1)
+    forward(2)
+    pass_forward(1)
+    sum_end(1)
+    sum_begin(2)
+    forward(3)
+    for k in range(4):
+        late(k)
+    quarters(dg, 0)
+    from_sibling([("sib_fx", 0), ("sib_fx", 1), ("sib_fy", 0), ("sib_fy", 1)])
+    quarters(sibling_of(dg), 0)
+    sum_end(2)
     last = len(partners) - 1
-    for stage in range(last - 1):
-        if stage:
-            greeted(stage)
+    for stage in range(3, last + 1):
+        greeted(stage)
         sum_begin(stage)
-        if stage == 0:
-            pass_forward(0)
+        if stage == 3:
+            pass_forward(2)
+        if stage == 4:
+            pass_forward(3)
         sum_end(stage)
-    sum_begin(last - 1)
-    late(0)
-    late(1)
-    pass_forward(1)
-    sum_end(last - 1)
-    sum_begin(last)
-    for k in range(2, 4):
-        late(k)
-    multiply(wall.at[dg], dg, 0, 2 * step)
-    multiply(wall.at[dg], dg, half, 2 * step)
-    sum_end(last)
     total = jnp.sum(jnp.sum(sums[last + 1], axis=0, keepdims=True), axis=1, keepdims=True)
     clip = jnp.minimum(1.0, 1.0 / jnp.sqrt(total + 1e-06))
 
@@ -377,14 +389,13 @@
             lanes_at = pl.ds(k * HD, HD)
             new_w[at, lanes_at] = (wv[at, lanes_at].astype(f32) - scale * g[at, lanes_at]).astype(bf16)
 
-    pass_forward(2)
-    pass_forward(3)
-    multiply(wall.at[dg], dg, 2 * step, 2 * step)
-    multiply(wall.at[dg], dg, half + 2 * step, 2 * step)
-    for k in range(4):
-        copies["sib_fx", k].wait_recv()
-        copies["sib_fy", k].wait_recv()
-    multiply(wall.at[sibling_of(dg)], sibling_of(dg))
+    if last < 3:
+        pass_forward(2)
+    if last < 4:
+        pass_forward(3)
+    quarters(dg, 2 * step)
+    from_sibling([("sib_fx", 2), ("sib_fx", 3), ("sib_fy", 2), ("sib_fy", 3)])
+    quarters(sibling_of(dg), 2 * step)
     for k in range(2):
         pass_late(k)
     multiply(wall.at[xn], xn, half, 2 * step)
@@ -488,7 +499,7 @@
             pltpu.VMEM((stages + 1, 8, HD), f32),
             pltpu.VMEM((stages, 8, HD), f32),
             pltpu.SemaphoreType.DMA((LOCALS,)),
-            pltpu.SemaphoreType.REGULAR((1 + len(zs),)),
+            pltpu.SemaphoreType.REGULAR((stages,)),
             pltpu.SemaphoreType.DMA((COPIES,)),
             pltpu.SemaphoreType.DMA((COPIES,)),
             pltpu.SemaphoreType.DMA((stages,)),

time: 80.9 us -> 78.5 us (0.970)
  Pallas kernels: 80.1 us -> 77.7 us
    pallas_call x1, Pallas kernels: 77.6 us -> 75.2 us  [shards_cube(): pl.pallas_call(functools.partial(exchange, zs), out_shape=(pltpu.VMEM((to...]
where the time goes in v3:
time: 78.5 us; the launch traced here: 78.3 us
  Pallas kernels  77.7 us (99%)
    pallas_call x1, Pallas kernels, shards_cube(): pl.pallas_call(functools.partial(exchange, zs), out_shape=(pltpu.VMEM((to...  75.2 us
    pallas_call x1, Pallas kernels, shards_cube(): pl.pallas_call(finish, out_shape=(jax.ShapeDtypeStruct((tokens, width), b...  2.49 us

profile of v3, /device:TPU:0, one launch (start us, length us, event | category | flops | bytes accessed | tf_op | source)
XLA Modules:
  0.0 78.3 jit_solution(13630740725871817296)
XLA Ops:
  0.6 75.2 %shard_map.76 = (bf16[512,4096]{1,0:T(8,128)(2,1)S(1)}, bf16[512,1024]{1,0:T(8,128)(2,1)S(1)}, f32[4,128]{1,0:T(4,128)S(1)}, bf16[512,1024]{1,0:T(8,128)(2,1)S(1)}, bf16[4,128,1024]{2,1,0:T(8,128)(2,1)S(1)}) custom-call(bf16[512,4096]{1,0:T(8,128)(2,1)} %hid.1, bf16[512,1024]{1,0:T(8,128)(2,1)} %w.1, f32[4,128]{1,0:T(4,128)} %bitcast.2, ...), custom_call_target="tpu_custom_call" | custom-call | tf_op jit(solution)/shard_map/pallas_call | solution.py:468
  75.8 2.5 %shard_map.77 = (bf16[512,4096]{1,0:T(8,128)(2,1)}, bf16[512,1024]{1,0:T(8,128)(2,1)}, f32[4,128]{1,0:T(4,128)}) custom-call(bf16[512,4096]{1,0:T(8,128)(2,1)S(1)} %get-tuple-element.11.ig_part, bf16[512,1024]{1,0:T(8,128)(2,1)S(1)} %get-tuple-element.12.kg, bf16[4,128,1024]{2,1,0:T(8,128)(2,1)S(1)} %get-tuple-element.13.tails, ...), custom_call_target="tpu_custom_call" | custom-call | tf_op jit(solution)/shard_map/pallas_call | solution.py:512

commit v4 on v2

--- a/solution.py
+++ b/solution.py
@@ -76,15 +76,17 @@
     return (input_grad, *update(owned, key_weight, key_state))
 
 
-COPIES = 64
-LOCALS = 8
-
-
-def exchange(zs, hid, w, state, cot, docs, ig, new_w, new_state, kg, tails, wv, states, cots, lengths, hh, kga, part, s1x, s1y, r1x, r1y, s2x, s2y, r2x, r2y, wall, g, squares, square_rows, sums, got, local, ready, send, recv, sum_send, sum_recv):
+OWN, HID, OWN_SIB, KG, RS1, RS2, SIB_OWN, FWD, LATE, CLOSE, SIB_FWD, SIB_LATE, SIB_CLOSE, SUM, PLANE, MP = (
+    0, 1, 2, 3, 4, 5, 6, 7, 9, 10, 13, 15, 16, 17, 18, 19)
+EARLY, MIDDLE, LAST, SUMS = 0, 1, 2, 3
+DOCS, COT, BIG, STATE = 0, 1, 2, 3
+
+
+def exchange(zs, hid, w, state, cot, docs, ig, new_w, new_state, kg, tails, wv, states, cots, lengths, hh, kga, part, s1x, s1y, r1x, r1y, s2x, s2y, r2x, r2y, wall, g, squares, square_rows, sums, got, whole, local, ready, send, recv):
     f32, bf16 = jnp.float32, jnp.bfloat16
     rows, kvw = wv.shape
     tokens = cots.shape[0]
-    half, step, cols = rows // 2, rows // 8, kvw // 2
+    half, step, cols = rows // 2, rows // 4, kvw // 2
     d = lax.axis_index("dp")
     core, xb, yb = lax.rem(d, 2), lax.rem(d // 2, 2), d // 4
     sib = d + 1 - 2 * core
@@ -104,69 +106,79 @@
     m = lax.axis_index("mp")
     partners = [{"dp": sib}]
     partners += [{"mp": m + bit - 2 * bit * lax.rem(m // bit, 2)} for bit in zs]
-    partners += [{"dp": xn}, {"dp": yn}]
-    late_half = [core] + [lax.rem(m // bit, 2) for bit in zs]
+    waits = {0: 1 - core, **{1 + j: core * lax.rem(m // bit, 2) for j, bit in enumerate(zs)}}
+    asks = {0: core, **{1 + j: core * (1 - lax.rem(m // bit, 2)) for j, bit in enumerate(zs)}}
 
     def signal(semaphore, to):
         pl.semaphore_signal(semaphore, inc=1, device_id=to, device_id_type=pl.DeviceIdType.MESH)
 
-    for to in partners[-2:]:
-        signal(barrier, to)
-    for j, upper in enumerate(late_half):
-
-        @pl.when(upper == 0)
+    for to in (xn, yn):
+        signal(barrier, {"dp": to})
+    for j, ask in asks.items():
+
+        @pl.when(ask == 1)
         def _(j=j):
             signal(barrier, partners[j])
 
     def greeted(j):
-        @pl.when(late_half[j] == 0)
+        @pl.when(asks[j] == 1)
         def _():
             pl.semaphore_wait(ready.at[j], 1)
 
-    locals_ = []
-
-    def fetch(src, dst):
-        copy = pltpu.make_async_copy(src, dst, local.at[len(locals_)])
-        locals_.append(copy)
-        copy.start()
-        return copy
-
-    small = [fetch(docs, lengths), fetch(cot, cots)]
-    own_hid = [fetch(hid.at[:, columns(block)], hh.at[i, pl.ds(0, tokens)]) for i, block in enumerate(blocks)]
-    own_w = fetch(w, wv)
-    own_state = fetch(state, states)
-    pl.semaphore_wait(barrier, 2 + sum(late_half))
-
-    copies = {}
-
-    def begin(name, src, dst, to):
-        place = len(copies)
-        copies[name] = pltpu.make_async_remote_copy(
+    pl.semaphore_wait(barrier, 2 + sum(waits.values()))
+
+    def on(which, act):
+        if which is None:
+            act()
+        else:
+            pl.when(core == which)(act)
+
+    def begin(place, sent, src, dst, to, by=None):
+        copy = pltpu.make_async_remote_copy(
             src_ref=src,
             dst_ref=dst,
-            send_sem=send.at[place],
+            send_sem=send.at[sent],
             recv_sem=recv.at[place],
-            device_id={"dp": to},
+            device_id=to if isinstance(to, dict) else {"dp": to},
             device_id_type=pl.DeviceIdType.MESH,
         )
-        copies[name].start()
+        on(by, copy.start)
+
+    def take(semaphore, like, by=None):
+        on(by, pltpu.make_async_copy(like, like, semaphore).wait)
+
+    def lines(count):
+        parts = next(n for n in range(1, wall.shape[0] + 1) if count % n == 0 and count // n <= rows)
+        return wall.at[pl.ds(0, parts), pl.ds(0, count // parts)]
+
+    def arrived(place, count, by=None):
+        take(recv.at[place], lines(count), by)
 
     first, second = pl.ds(0, half), pl.ds(half, half)
-    begin("own_x", w.at[first], wall.at[d, first], xn)
-    begin("own_y", w.at[second], wall.at[d, second], yn)
-    for j, upper in enumerate(late_half):
-
-        @pl.when(upper == 1)
+    begin(OWN, EARLY, w.at[first], wall.at[d, first], xn)
+    begin(OWN, EARLY, w.at[second], wall.at[d, second], yn)
+    for j, wait in waits.items():
+
+        @pl.when(wait == 1)
         def _(j=j):
             signal(ready.at[j], partners[j])
 
+    def fetch(place, src, dst):
+        pltpu.make_async_copy(src, dst, local.at[place]).start()
+
+    fetch(DOCS, docs, lengths)
+    fetch(COT, cot, cots)
+    for i, block in enumerate(blocks):
+        fetch(BIG, hid.at[:, columns(block)], hh.at[i, pl.ds(0, tokens)])
+    fetch(BIG, w, wv)
+    fetch(STATE, state, states)
     greeted(0)
     for i, block in enumerate(blocks):
-        begin(("hid", i), hid.at[:, columns(sibling_of(block))], hh.at[i, pl.ds(tokens, tokens)], sib)
-    begin("own_sib", w, wall.at[d], sib)
-
-    for copy in small:
-        copy.wait()
+        begin(HID, EARLY, hid.at[:, columns(sibling_of(block))], hh.at[i, pl.ds(tokens, tokens)], sib)
+    begin(OWN_SIB, EARLY, w, wall.at[d], sib)
+
+    take(local.at[DOCS], lengths)
+    take(local.at[COT], cots)
     slab = LEN // 4
     pair = lax.rem(lax.broadcasted_iota(jnp.int32, (1, HD), 1), HD // 2).astype(f32)
     frequency = jnp.exp(-(2.0 * pair / HD) * jnp.log(jnp.float32(500000.0)))
@@ -196,11 +208,10 @@
                 kg[at, head] = turned
 
     mine = pl.ds(0, tokens)
-    begin("kg", kga.at[mine], kga.at[pl.ds(tokens, tokens)], sib)
-    for copy in own_hid:
-        copy.wait()
-    own_w.wait()
-    own_state.wait()
+    begin(KG, EARLY, kga.at[mine], kga.at[pl.ds(tokens, tokens)], sib)
+    block_lines = tokens * rows // kvw
+    take(local.at[BIG], lines(4 * block_lines + rows))
+    take(local.at[STATE], states)
 
     def multiply(weights, block, at=0, size=rows, tile=half):
         tile = min(tile, size)
@@ -211,10 +222,9 @@
                 kga[mine, :], weights[pl.ds(pl.multiple_of(at + t * tile, tile), tile), :], (((1,), (1,)), ((), ())), preferred_element_type=f32
             ).astype(bf16)
 
-    copies["kg"].wait_recv()
+    arrived(KG, tokens)
+    arrived(HID, 4 * block_lines)
     for i in range(4):
-        copies["hid", i].wait_recv()
-
         @pl.loop(0, 2)
         def _(t, i=i):
             at = pl.ds(pl.multiple_of(t * half, half), half)
@@ -233,85 +243,91 @@
                 part[3, at, :] = total[:, cols:]
 
         if i == 0:
-            begin(("rs1_x", 0), s1x.at[0], r1x.at[0], xn)
-            begin(("rs1_y", 0), s1y.at[0], r1y.at[0], yn)
+            begin(RS1, EARLY, s1x.at[0], r1x.at[0], xn)
+            begin(RS1, EARLY, s1y.at[0], r1y.at[0], yn)
         if i == 1:
-            begin(("rs1_x", 1), s1x.at[1], r1x.at[1], xn)
+            begin(RS2, EARLY, s1x.at[1], r1x.at[1], xn)
         if i == 2:
-            begin(("rs1_y", 1), s1y.at[1], r1y.at[1], yn)
+            begin(RS2, EARLY, s1y.at[1], r1y.at[1], yn)
 
     multiply(wv, d)
-    copies["own_sib"].wait_recv()
+    arrived(OWN_SIB, rows)
     multiply(wall.at[sib], sib)
-    copies["own_x"].wait_recv()
-    begin("sib_x", wall.at[xn, first], wall.at[xn, first], sib)
-    copies["own_y"].wait_recv()
-    begin("sib_y", wall.at[yn, second], wall.at[yn, second], sib)
+    arrived(OWN, rows)
+    begin(SIB_OWN, MIDDLE, wall.at[xn, first], wall.at[xn, first], sib)
+    begin(SIB_OWN, MIDDLE, wall.at[yn, second], wall.at[yn, second], sib)
     multiply(wall.at[xn], xn, 0, half)
     multiply(wall.at[yn], yn, half, half)
 
-    copies["rs1_x", 0].wait_recv()
+    arrived(RS1, rows)
 
     @pl.loop(0, 4)
     def _(t):
         at = pl.ds(pl.multiple_of(t * (rows // 4), rows // 4), rows // 4)
         s2y[at, :] = (part[1, at, :] + r1x[0, at, :].astype(f32)).astype(bf16)
 
-    begin("rs2_y", s2y, r2y, yn)
-    copies["rs1_y", 0].wait_recv()
+    begin(RS2, EARLY, s2y, r2y, yn)
 
     @pl.loop(0, 4)
     def _(t):
         at = pl.ds(pl.multiple_of(t * (rows // 4), rows // 4), rows // 4)
         s2x[at, :] = (part[0, at, :] + r1y[0, at, :].astype(f32)).astype(bf16)
 
-    begin("rs2_x", s2x, r2x, xn)
+    begin(RS2, EARLY, s2x, r2x, xn)
+
+    def spans(k):
+        return pl.ds(k * step, step), pl.ds(half + k * step, step)
 
     def forward(k):
-        low, high = pl.ds(k * step, step), pl.ds(half + k * step, step)
-        begin(("fwd_x", k), wall.at[yn, high], wall.at[yn, high], xn)
-        begin(("fwd_y", k), wall.at[xn, low], wall.at[xn, low], yn)
-
-    def late(k):
-        low, high = pl.ds(k * step, step), pl.ds(half + k * step, step)
-        to_x, to_y = wall.at[d, high], wall.at[d, low]
-        if k >= 2:
-            to_x, to_y = (tails.at[i, pl.ds((k - 2) * step, step)] for i in range(2))
-        begin(("late_x", k), wv.at[high], to_x, xn)
-        begin(("late_y", k), wv.at[low], to_y, yn)
+        low, high = spans(k)
+        begin(FWD + k, MIDDLE, wall.at[yn, high], wall.at[yn, high], xn)
+        begin(FWD + k, MIDDLE, wall.at[xn, low], wall.at[xn, low], yn)
 
     def pass_forward(k):
-        low, high = pl.ds(k * step, step), pl.ds(half + k * step, step)
-        copies["fwd_x", k].wait_recv()
-        begin(("sib_fx", k), wall.at[dg, high], wall.at[dg, high], sib)
-        copies["fwd_y", k].wait_recv()
-        begin(("sib_fy", k), wall.at[dg, low], wall.at[dg, low], sib)
-
-    def pass_late(k):
-        low, high = pl.ds(k * step, step), pl.ds(half + k * step, step)
-        at = pl.ds((k - 2) * step, step)
-        copies["late_x", k].wait_recv()
-        if k < 2:
-            begin(("sib_lx", k), wall.at[xn, high], wall.at[xn, high], sib)
-        else:
-            begin(("sib_lx", k), tails.at[0, at], tails.at[2, at], sib)
-        copies["late_y", k].wait_recv()
-        if k < 2:
-            begin(("sib_ly", k), wall.at[yn, low], wall.at[yn, low], sib)
-        else:
-            begin(("sib_ly", k), tails.at[1, at], tails.at[3, at], sib)
-
-    for k in range(4):
-        forward(k)
-    copies["sib_x"].wait_recv()
-    copies["sib_y"].wait_recv()
+        arrived(FWD + k, 2 * step)
+        for span in spans(k):
+            begin(SIB_FWD + k, MIDDLE, wall.at[dg, span], wall.at[dg, span], sib)
+
+    def late():
+        low, high = spans(0)
+        begin(LATE, MIDDLE, wv.at[high], wall.at[d, high], xn)
+        begin(LATE, MIDDLE, wv.at[low], wall.at[d, low], yn)
+
+    def pass_late():
+        low, high = spans(0)
+        arrived(LATE, 2 * step)
+        begin(SIB_LATE, MIDDLE, wall.at[xn, high], wall.at[xn, high], sib)
+        begin(SIB_LATE, MIDDLE, wall.at[yn, low], wall.at[yn, low], sib)
+
+    moved = step // 4
+    pieces = (
+        (None, 0, 0, step // 2),
+        (0, 1, step // 2, step // 2 - moved),
+        (1, 1, step // 2, step // 2),
+        (1, 2, step - moved, moved),
+    )
+
+    def close():
+        for by, place, at, size in pieces:
+            source, slot = (wall.at[sib], 2) if place == 2 else (wv, 0)
+            for j, base, to in ((0, rows, xn), (1, half, yn)):
+                src = source.at[pl.ds(base - step + at, size)]
+                begin(CLOSE + place, LAST, src, tails.at[slot + j, pl.ds(at, size)], to, by)
+
+    def pass_close():
+        for by, place, at, size in pieces:
+            slot = 2 if place == 2 else 0
+            arrived(CLOSE + place, 2 * size, by)
+            for j in range(2):
+                part_of = pl.ds(at, size)
+                begin(SIB_CLOSE, LAST, tails.at[slot + j, part_of], tails.at[2 - slot + j, part_of], sib, by)
+
+    forward(0)
+    arrived(SIB_OWN, rows)
     multiply(wall.at[sibling_of(xn)], sibling_of(xn), 0, half)
     multiply(wall.at[sibling_of(yn)], sibling_of(yn), half, half)
 
-    copies["rs1_x", 1].wait_recv()
-    copies["rs1_y", 1].wait_recv()
-    copies["rs2_x"].wait_recv()
-    copies["rs2_y"].wait_recv()
+    arrived(RS2, 2 * rows)
 
     sums[0] = jnp.zeros_like(sums[0])
     for t in range(rows // HD):
@@ -328,42 +344,48 @@
         square_rows[pl.ds(t, 1), :] = jnp.sum(lanes.T, axis=0, keepdims=True)
         sums[0] += jnp.sum(lanes.reshape(HD // 8, 8, HD), axis=0)
 
-    def sum_begin(stage):
-        copy = pltpu.make_async_remote_copy(
-            src_ref=sums.at[stage],
-            dst_ref=got.at[stage],
-            send_sem=sum_send.at[stage],
-            recv_sem=sum_recv.at[stage],
-            device_id=partners[stage],
-            device_id_type=pl.DeviceIdType.MESH,
-        )
-        copies["sum", stage] = copy
-        copy.start()
-
-    def sum_end(stage):
-        copies["sum", stage].wait_recv()
-        sums[stage + 1] = sums[stage] + got[stage]
-
-    last = len(partners) - 1
-    for stage in range(last - 1):
-        if stage:
-            greeted(stage)
-        sum_begin(stage)
-        if stage == 0:
-            pass_forward(0)
-        sum_end(stage)
-    sum_begin(last - 1)
-    late(0)
-    late(1)
-    pass_forward(1)
-    sum_end(last - 1)
-    sum_begin(last)
-    for k in range(2, 4):
-        late(k)
-    multiply(wall.at[dg], dg, 0, 2 * step)
-    multiply(wall.at[dg], dg, half, 2 * step)
-    sum_end(last)
-    total = jnp.sum(jnp.sum(sums[last + 1], axis=0, keepdims=True), axis=1, keepdims=True)
+    def quarters(block, at):
+        multiply(wall.at[block], block, at, step)
+        multiply(wall.at[block], block, half + at, step)
+
+    last = 2 + len(zs)
+
+    def add(into, places):
+        @pl.when(core == 1)
+        def _():
+            if len(places) == 1:
+                sums[into] = sums[into - 1] + got[places[0]]
+            else:
+                sums[into] = (sums[into - 1] + got[places[0]]) + (got[places[1]] + got[places[2]])
+
+    begin(SUM, SUMS, sums.at[0], got.at[0], sib, 0)
+    take(recv.at[SUM], whole, 1)
+    add(1, [0])
+    for j, to in enumerate((xn, yn, dg)):
+        begin(PLANE, SUMS, sums.at[1], got.at[1 + j], to, 1)
+    forward(1)
+    late()
+    close()
+    pass_forward(0)
+    quarters(dg, 0)
+    take(recv.at[PLANE], got.at[pl.ds(1, 3)], 1)
+    add(2, [1, 2, 3])
+    for j in range(len(zs)):
+        greeted(1 + j)
+        begin(MP + j, SUMS, sums.at[2 + j], got.at[4 + j], partners[1 + j], 1)
+        if j == 0:
+            arrived(SIB_FWD, 2 * step)
+            quarters(sibling_of(dg), 0)
+        take(recv.at[MP + j], whole, 1)
+        add(3 + j, [4 + j])
+
+    @pl.when(core == 1)
+    def _():
+        whole[...] = sums[last]
+
+    begin(SUM, SUMS, sums.at[last], whole, sib, 1)
+    take(recv.at[SUM], whole, 0)
+    total = jnp.sum(jnp.sum(whole[...], axis=0, keepdims=True), axis=1, keepdims=True)
     clip = jnp.minimum(1.0, 1.0 / jnp.sqrt(total + 1e-06))
 
     for t in range(rows // HD):
@@ -377,31 +399,26 @@
             lanes_at = pl.ds(k * HD, HD)
             new_w[at, lanes_at] = (wv[at, lanes_at].astype(f32) - scale * g[at, lanes_at]).astype(bf16)
 
-    pass_forward(2)
-    pass_forward(3)
-    multiply(wall.at[dg], dg, 2 * step, 2 * step)
-    multiply(wall.at[dg], dg, half + 2 * step, 2 * step)
-    for k in range(4):
-        copies["sib_fx", k].wait_recv()
-        copies["sib_fy", k].wait_recv()
-    multiply(wall.at[sibling_of(dg)], sibling_of(dg))
-    for k in range(2):
-        pass_late(k)
-    multiply(wall.at[xn], xn, half, 2 * step)
-    multiply(wall.at[yn], yn, 0, 2 * step)
-    for k in range(2):
-        copies["sib_lx", k].wait_recv()
-        copies["sib_ly", k].wait_recv()
-    multiply(wall.at[sibling_of(xn)], sibling_of(xn), half, 2 * step)
-    multiply(wall.at[sibling_of(yn)], sibling_of(yn), 0, 2 * step)
-    for k in range(2, 4):
-        pass_late(k)
-    for k in range(2, 4):
-        copies["sib_lx", k].wait_recv()
-        copies["sib_ly", k].wait_recv()
-
-    for copy in copies.values():
-        copy.wait_send()
+    pass_forward(1)
+    quarters(dg, step)
+    arrived(SIB_FWD + 1, 2 * step)
+    quarters(sibling_of(dg), step)
+    pass_late()
+    multiply(wall.at[xn], xn, half, step)
+    multiply(wall.at[yn], yn, 0, step)
+    arrived(SIB_LATE, 2 * step)
+    multiply(wall.at[sibling_of(xn)], sibling_of(xn), half, step)
+    multiply(wall.at[sibling_of(yn)], sibling_of(yn), 0, step)
+    pass_close()
+    counts = [2 * sum(size for by, _, _, size in pieces if by in (None, which)) for which in range(2)]
+    for which in range(2):
+        arrived(SIB_CLOSE, counts[1 - which], which)
+    take(send.at[EARLY], lines(tokens + 5 * rows + 4 * block_lines))
+    take(send.at[MIDDLE], lines(4 * rows))
+    for which in range(2):
+        take(send.at[LAST], lines(2 * counts[which]), which)
+    take(send.at[SUMS], whole, 0)
+    take(send.at[SUMS], got.at[pl.ds(0, 4 + len(zs))], 1)
 
 
 def finish(ig_part, kg, tails, w_part, state_part, ig, new_w, new_state, last, sems):
@@ -413,12 +430,11 @@
     yn = d + 4 - 8 * yb
     dg = xn + 4 - 8 * yb
     flip = 1 - 2 * core
-    copies = []
-
-    def put(src, dst):
-        copy = pltpu.make_async_copy(src, dst, sems.at[len(copies)])
-        copies.append(copy)
+
+    def put(src, dst, place=0):
+        copy = pltpu.make_async_copy(src, dst, sems.at[place])
         copy.start()
+        return copy
 
     def ready(block, at, size):
         where = pl.ds(pl.multiple_of(block * rows + at, HD), size)
@@ -432,15 +448,15 @@
     for owner in (yn, yn + flip):
         ready(owner, 0, half - tail)
         ready(owner, half, half)
-    put(w_part, new_w)
-    put(state_part, new_state)
+    others = put(w_part, new_w, 1), put(state_part, new_state, 2)
     for i, owner in enumerate((xn, yn, xn + flip, yn + flip)):
         last[i] = lax.dot_general(
             kg[...], tails[i], (((1,), (1,)), ((), ())), preferred_element_type=jnp.float32
         ).astype(jnp.bfloat16)
         at = (half if i % 2 else rows) - tail
         put(last.at[i], ig.at[:, pl.ds(pl.multiple_of(owner * rows + at, HD), tail)])
-    for copy in copies:
+    pltpu.make_async_copy(ig_part, ig, sems.at[0]).wait()
+    for copy in others:
         copy.wait()
 
 
@@ -485,14 +501,13 @@
             pltpu.VMEM((rows, kvw), f32),
             pltpu.VMEM((rows, 1), f32),
             pltpu.VMEM((groups, HD), f32),
+            pltpu.VMEM((stages, 8, HD), f32),
             pltpu.VMEM((stages + 1, 8, HD), f32),
-            pltpu.VMEM((stages, 8, HD), f32),
-            pltpu.SemaphoreType.DMA((LOCALS,)),
+            pltpu.VMEM((8, HD), f32),
+            pltpu.SemaphoreType.DMA((STATE + 1,)),
             pltpu.SemaphoreType.REGULAR((1 + len(zs),)),
-            pltpu.SemaphoreType.DMA((COPIES,)),
-            pltpu.SemaphoreType.DMA((COPIES,)),
-            pltpu.SemaphoreType.DMA((stages,)),
-            pltpu.SemaphoreType.DMA((stages,)),
+            pltpu.SemaphoreType.DMA((SUMS + 1,)),
+            pltpu.SemaphoreType.DMA((MP + len(zs),)),
         ],
         compiler_params=pltpu.CompilerParams(
             collective_id=0, has_side_effects=True, vmem_limit_bytes=56 * 1024 * 1024
@@ -507,7 +522,7 @@
         ),
         in_specs=[held, vmem, vmem, held, held],
         out_specs=(held,) * 3,
-        scratch_shapes=[pltpu.VMEM((4, tokens, tail), bf16), pltpu.SemaphoreType.DMA((16,))],
+        scratch_shapes=[pltpu.VMEM((4, tokens, tail), bf16), pltpu.SemaphoreType.DMA((3,))],
         compiler_params=pltpu.CompilerParams(vmem_limit_bytes=4 * 1024 * 1024),
     )(parts[0], kg, tails, *parts[1:])
     return input_grad, new_weight, new_state.reshape(rows)

time: 80.9 us -> 76.8 us (0.949)
  Pallas kernels: 80.1 us -> 76 us
    pallas_call x1, Pallas kernels: 77.6 us -> 73.6 us  [shards_cube(): pl.pallas_call(functools.partial(exchange, zs), out_shape=(pltpu.VMEM((to...]
where the time goes in v4:
time: 76.8 us; the launch traced here: 76.6 us
  Pallas kernels  76 us (99%)
    pallas_call x1, Pallas kernels, shards_cube(): pl.pallas_call(functools.partial(exchange, zs), out_shape=(pltpu.VMEM((to...  73.6 us
    pallas_call x1, Pallas kernels, shards_cube(): pl.pallas_call(finish, out_shape=(jax.ShapeDtypeStruct((tokens, width), b...  2.38 us

profile of v4, /device:TPU:0, one launch (start us, length us, event | category | flops | bytes accessed | tf_op | source)
XLA Modules:
  0.0 76.6 jit_solution(11616253620256223815)
XLA Ops:
  0.6 73.6 %shard_map.76 = (bf16[512,4096]{1,0:T(8,128)(2,1)S(1)}, bf16[512,1024]{1,0:T(8,128)(2,1)S(1)}, f32[4,128]{1,0:T(4,128)S(1)}, bf16[512,1024]{1,0:T(8,128)(2,1)S(1)}, bf16[4,128,1024]{2,1,0:T(8,128)(2,1)S(1)}) custom-call(bf16[512,4096]{1,0:T(8,128)(2,1)} %hid.1, bf16[512,1024]{1,0:T(8,128)(2,1)} %w.1, f32[4,128]{1,0:T(4,128)} %bitcast.2, ...), custom_call_target="tpu_custom_call" | custom-call | tf_op jit(solution)/shard_map/pallas_call | solution.py:473
  74.3 2.4 %shard_map.77 = (bf16[512,4096]{1,0:T(8,128)(2,1)}, bf16[512,1024]{1,0:T(8,128)(2,1)}, f32[4,128]{1,0:T(4,128)}) custom-call(bf16[512,4096]{1,0:T(8,128)(2,1)S(1)} %get-tuple-element.11.ig_part, bf16[512,1024]{1,0:T(8,128)(2,1)S(1)} %get-tuple-element.12.kg, bf16[4,128,1024]{2,1,0:T(8,128)(2,1)S(1)} %get-tuple-element.13.tails, ...), custom_call_target="tpu_custom_call" | custom-call | tf_op jit(solution)/shard_map/pallas_call | solution.py:516
